TPU v7x, 32 devices: a whole 2x2x4 slice. The times are simulated.
32 devices in a mesh: grp: 8 (over y, x, core), rep: 4 (over z).
Axes of the slice: x: 2, y: 2, z: 4, core: 2. Of those that a mesh axis runs over, the one named last changes fastest.
Arguments:
- momentum: bfloat16 [256, 4096], P(('grp', 'rep')), may hold values from -6 to 6
- picked: int32 [256, 32], P(('grp', 'rep')), may hold values from 0 to 4095, as said below
- owner_span_order: int32 [8], replicated, may hold values from 0 to 7, each once
Outputs:
- update: bfloat16 [8, 4096], replicated
- residual_momentum: bfloat16 [256, 4096], P(('grp', 'rep'))
Inputs may be any that keep to these rules, and one draw needn't show every extreme that they name: `picked`: the 32 numbers of a row are different. `owner_span_order`: each span stands once.
All inputs are finite; a program needn't handle non-finite values.
Results may differ from a plain program's by a relative error of at most 0.013.
Values may be sent and summed in bfloat16 or wider, within the bound.
A program may use at most 64 MiB of HBM per device.

v0:
```python
import math

import functools

import jax
import jax.numpy as jnp
import numpy as np
from jax import lax
from jax.experimental import pallas as pl
from jax.experimental.pallas import tpu as pltpu
from jax.sharding import PartitionSpec as P

BLOCK = 64
TOPK = 32
CH_OWN = 1


def dct_cosines(points):
    freq = jnp.arange(points, dtype=jnp.float32)[:, None]
    place = jnp.arange(points, dtype=jnp.float32)[None, :]
    values = jnp.cos(jnp.pi * (2.0 * place + 1.0) * freq / (2.0 * points)) * jnp.sqrt(2.0 / points)
    values = values.at[0].multiply(jnp.sqrt(0.5))
    rounded = lax.optimization_barrier(values.astype(jnp.bfloat16))
    return rounded.astype(jnp.float32)


def forward(square_low, cosines, cos_low):
    half = jnp.einsum("cab,jb->caj", square_low, cos_low, preferred_element_type=jnp.float32)
    return jnp.einsum("ia,caj->cij", cosines, half, precision=lax.Precision.HIGHEST)


def decode(dense_matrix, cosines):
    square = dense_matrix.reshape(dense_matrix.shape[0], BLOCK, BLOCK)
    half = jnp.einsum("cij,jb->cib", square, cosines, precision=lax.Precision.HIGHEST)
    full = jnp.einsum("ia,cib->cab", cosines, half, precision=lax.Precision.HIGHEST)
    return full.reshape(dense_matrix.shape[0], BLOCK * BLOCK)


def decode_sparse(dense_low, cosines, cos_low):
    square = dense_low.reshape(dense_low.shape[0], BLOCK, BLOCK)
    half = jnp.einsum("cij,jb->cib", square, cos_low, preferred_element_type=jnp.float32)
    full = jnp.einsum("ia,cib->cab", cosines, half, precision=lax.Precision.HIGHEST)
    return full.reshape(dense_low.shape[0], BLOCK * BLOCK)


def densify(values, spots):
    entries, columns = values.shape
    per_step = math.gcd(entries, max(1, 65536 // columns))
    positions = jnp.arange(BLOCK, dtype=jnp.int32)

    def one_block(pieces):
        block_values, block_spots = pieces
        zeros = jnp.zeros_like(block_values)
        row_onehot = jnp.where(
            (block_spots // BLOCK)[:, None, :] == positions[None, :, None],
            block_values[:, None, :],
            zeros[:, None, :],
        )
        column_onehot = ((block_spots % BLOCK)[:, None, :] == positions[None, :, None]).astype(
            jnp.bfloat16
        )
        dense_matrix = jnp.einsum(
            "bcy,bzy->bcz", row_onehot, column_onehot, preferred_element_type=jnp.float32
        )
        return dense_matrix.reshape(per_step, BLOCK * BLOCK)

    stacked = lax.map(
        one_block,
        (
            values.reshape(entries // per_step, per_step, columns),
            spots.reshape(entries // per_step, per_step, columns),
        ),
    )
    return stacked.reshape(entries, BLOCK * BLOCK)


def owner_sum(received):
    values, spots = received
    return densify(values[0], spots[0])


def local_large(momentum, picked, owner_span_order):
    cosines = dct_cosines(BLOCK)
    cos_low = cosines.astype(jnp.bfloat16)
    owners = lax.axis_size("grp")
    span_count = momentum.shape[0]
    square_low = momentum.reshape(span_count, BLOCK, BLOCK)
    transform_coefficients = forward(square_low, cosines, cos_low).reshape(
        span_count, BLOCK * BLOCK
    )
    chosen = jnp.take_along_axis(transform_coefficients, picked, axis=1).astype(jnp.bfloat16)
    own_dense = densify(chosen, picked).astype(jnp.bfloat16)
    residual_momentum = (
        momentum.astype(jnp.float32) - decode_sparse(own_dense, cosines, cos_low)
    ).astype(jnp.bfloat16)
    slot_values = jnp.take(chosen, owner_span_order, axis=0)
    slot_spots = jnp.take(picked, owner_span_order, axis=0)
    shaped = (slot_values.reshape(owners, CH_OWN, TOPK), slot_spots.reshape(owners, CH_OWN, TOPK))
    partial_sum = owner_sum(
        (
            lax.all_to_all(shaped[0], "grp", split_axis=0, concat_axis=2, tiled=True),
            lax.all_to_all(shaped[1], "grp", split_axis=0, concat_axis=2, tiled=True),
        )
    )
    partial_sum = lax.psum(partial_sum, "rep")
    my_share = decode(partial_sum, cosines).astype(jnp.bfloat16)
    update = lax.all_gather(my_share, "grp", axis=0, tiled=True)
    return (update, residual_momentum)


LANES = 128
GATHER_BYTES = 2**20


def cosine_table():
    freq = np.arange(BLOCK, dtype=np.float64)[:, None]
    place = np.arange(BLOCK, dtype=np.float64)[None, :]
    values = np.cos(np.pi * (2 * place + 1) * freq / (2 * BLOCK)) * np.sqrt(2 / BLOCK)
    values[0] *= np.sqrt(0.5)
    return values.astype(np.float32)


def contract_lanes(left, right):
    return lax.dot_general(
        left, right, (((1,), (1,)), ((), ())), preferred_element_type=jnp.float32
    )


def matmul(left, right):
    return jnp.dot(left, right, preferred_element_type=jnp.float32)


def split(value):
    high = value.astype(jnp.bfloat16)
    return high, (value - high.astype(jnp.float32)).astype(jnp.bfloat16)


def exchange_kernel(
    groups,
    planes,
    order_hbm,
    momentum_hbm,
    picked_hbm,
    rows_hbm,
    cols_hbm,
    twice_hbm,
    pairs_hbm,
    update_ref,
    residual_ref,
    order_ref,
    momentum_ref,
    picked_ref,
    rows_ref,
    cols_ref,
    twice_ref,
    pairs_ref,
    box,
    turned,
    dense,
    decoded,
    load_sem,
    send_sem,
    recv_sem,
):
    sources = (picked_hbm, cols_hbm, rows_hbm, momentum_hbm, twice_hbm, pairs_hbm, order_hbm)
    targets = (picked_ref, cols_ref, rows_ref, momentum_ref, twice_ref, pairs_ref, order_ref)
    loads = [
        pltpu.make_async_copy(source, target, load_sem.at[n])
        for n, (source, target) in enumerate(zip(sources, targets))
    ]
    for load in loads:
        load.start()
    spans = momentum_ref.shape[0]
    entries = spans * TOPK
    chunks = BLOCK * BLOCK // LANES
    in_tile = LANES // TOPK
    tiles = entries // LANES
    devices = groups * planes
    my_group, my_plane = lax.axis_index("grp"), lax.axis_index("rep")
    group_of = [lax.rem(my_group + step, groups) for step in range(groups)]
    plane_of = [lax.rem(my_plane + step, planes) for step in range(planes)]

    def peer(plane, group):
        return {"grp": group_of[group], "rep": plane_of[plane]}

    others = [(z, g) for z in range(planes) for g in range(groups) if z or g]
    far_first = [o for o in others if o[0]] + [o for o in others if not o[0]]
    barrier = pltpu.get_barrier_semaphore()
    for z, g in far_first:
        pl.semaphore_signal(barrier, inc=1, device_id=peer(z, g), device_id_type=pl.DeviceIdType.MESH)

    loads[0].wait()
    lane = lax.broadcasted_iota(jnp.int32, (spans, entries), 1)
    mine = (lane // TOPK) == lax.broadcasted_iota(jnp.int32, (spans, entries), 0)
    spread = jnp.concatenate([picked_ref[...]] * spans, axis=1)
    spots = jnp.sum(jnp.where(mine, spread, 0), axis=0, keepdims=True)
    freq = lax.broadcasted_iota(jnp.int32, (BLOCK, entries), 0)
    row_spot, col_spot = spots // BLOCK, spots % BLOCK
    one_row = jnp.where(freq == row_spot, 1.0, 0.0).astype(jnp.bfloat16)
    one_col = jnp.where(freq == col_spot, 1.0, 0.0).astype(jnp.bfloat16)
    half_rows = chunks * spans
    for load in loads[1:]:
        load.wait()
    wave = matmul(cols_ref[...], one_col).astype(jnp.bfloat16)
    blank = jnp.zeros_like(wave)
    waves = (jnp.concatenate([wave, blank], axis=0), jnp.concatenate([blank, wave], axis=0))
    momentum = jnp.concatenate(
        [momentum_ref[:, k * LANES : (k + 1) * LANES].astype(jnp.float32) for k in range(chunks)],
        axis=0,
    )
    momentum_low = momentum.astype(jnp.bfloat16)
    total = jnp.zeros((spans, entries), jnp.float32)
    row_waves = []
    for p in range(2):
        row_wave = matmul(rows_ref[p * half_rows : (p + 1) * half_rows, :], one_row)
        row_waves.append(row_wave)
        product = row_wave * matmul(momentum_low, waves[p])
        total += jnp.sum(product.reshape(chunks, spans, entries), axis=0)
    chosen = jnp.sum(jnp.where(mine, total, 0.0), axis=0, keepdims=True)
    chosen_low = chosen.astype(jnp.bfloat16)
    chosen = chosen_low.astype(jnp.float32)

    def by_tile(row):
        return jnp.concatenate(
            [row[:, h * LANES : (h + 1) * LANES] for h in range(tiles)], axis=0
        )

    def store_residual():
        correction = jnp.zeros((half_rows, LANES), jnp.float32)
        scaled = jnp.where(mine, chosen, 0.0)
        for p in range(2):
            weight = row_waves[p].reshape(chunks, spans, entries) * scaled[None]
            for part in split(weight.reshape(half_rows, entries)):
                correction += contract_lanes(part, waves[p])
        residual = momentum - correction
        for k in range(chunks):
            residual_ref[:, k * LANES : (k + 1) * LANES] = residual[
                k * spans : (k + 1) * spans
            ].astype(jnp.bfloat16)

    parts = [by_tile(part) for part in (chosen, row_spot.astype(jnp.float32), col_spot.astype(jnp.float32))]
    for turn in range(in_tile):
        turned[turn] = jnp.concatenate(
            [pltpu.roll(part, turn * TOPK, 1).astype(jnp.bfloat16) for part in parts], axis=1
        )
    box[0] = jnp.concatenate([part.astype(jnp.bfloat16) for part in parts], axis=1)
    pl.when(my_plane == 0)(store_residual)
    pl.semaphore_wait(barrier, devices - 1)
    copies = []
    for z, g in far_first:
        copy = pltpu.make_async_remote_copy(
            src_ref=turned.at[g % in_tile],
            dst_ref=box.at[z * groups + g],
            send_sem=send_sem,
            recv_sem=recv_sem.at[z],
            device_id=peer(z, g),
            device_id_type=pl.DeviceIdType.MESH,
        )
        copy.start()
        copies.append(copy)

    block = lax.broadcasted_iota(jnp.int32, (tiles, LANES), 1) // TOPK
    taken = [block == turn for turn in range(in_tile)]
    freq = lax.broadcasted_iota(jnp.int32, (BLOCK, groups * TOPK), 0)
    freq = freq.astype(jnp.float32).astype(jnp.bfloat16)
    one, zero = jnp.ones((), jnp.bfloat16), jnp.zeros((), jnp.bfloat16)

    def span_rows(rows, c):
        picks = []
        for first in range(0, groups, in_tile):
            row = rows[first]
            for turn in range(1, in_tile):
                row = jnp.where(taken[(c + turn) % in_tile], rows[first + turn], row)
            picks.append(row)
        return jnp.concatenate(picks, axis=1)

    sums = [None] * spans
    for z in range(planes):
        first = 1 if z == 0 else 0
        landed = box.at[pl.ds(z * groups + first, groups - first)]
        pltpu.make_async_copy(landed, landed, recv_sem.at[z]).wait()
        slots = [box[z * groups + g].astype(jnp.float32) for g in range(groups)]
        values, rows, columns = (
            [slot[:, n * LANES : (n + 1) * LANES] for slot in slots] for n in range(3)
        )
        for c in range(in_tile):
            value, row, column = (
                span_rows(part, c).astype(jnp.bfloat16) for part in (values, rows, columns)
            )
            for h in range(tiles):
                left = jnp.where(freq == row[h : h + 1], one, zero)
                right = jnp.where(freq == column[h : h + 1], value[h : h + 1], zero)
                part = contract_lanes(left, right)
                span = h * in_tile + c
                sums[span] = part if z == 0 else sums[span] + part
    for span in range(spans):
        dense[span] = matmul(sums[span].astype(jnp.bfloat16), twice_ref[...])
    lower = lax.broadcasted_iota(jnp.int32, (chunks, LANES), 1) < BLOCK
    for s in range(spans):
        full = matmul(pairs_ref[...], dense[order_ref[s]].astype(jnp.bfloat16))
        decoded[pl.ds(s, chunks, stride=spans), :] = jnp.where(
            lower, full[:chunks], full[chunks:]
        )
    for k in range(chunks):
        update_ref[:, k * LANES : (k + 1) * LANES] = decoded[
            k * spans : (k + 1) * spans, :
        ].astype(jnp.bfloat16)
    pl.when(my_plane != 0)(store_residual)
    for copy in copies:
        copy.wait_send()


def store_kernel(update_ref, residual_ref, update_hbm, residual_hbm, sem):
    stores = [
        pltpu.make_async_copy(residual_ref, residual_hbm, sem.at[0]),
        pltpu.make_async_copy(update_ref, update_hbm, sem.at[1]),
    ]
    for store in stores:
        store.start()
    for store in stores:
        store.wait()


def local_small(groups, planes, momentum, picked, owner_span_order):
    spans = momentum.shape[0]
    chunks = BLOCK * BLOCK // LANES
    table = cosine_table()
    by_pair = table.T.reshape(chunks, 2, BLOCK)
    rows = np.repeat(by_pair.transpose(1, 0, 2), spans, axis=1).reshape(-1, BLOCK)
    constants = [rows, table.T, np.concatenate([table, table], axis=1), by_pair.transpose(1, 0, 2).reshape(-1, BLOCK)]
    constants = [jnp.asarray(constant, dtype=jnp.bfloat16) for constant in constants]
    operands = [owner_span_order, momentum, picked, *constants]
    anywhere = pl.BlockSpec(memory_space=pl.ANY)
    vmem = pl.BlockSpec(memory_space=pltpu.VMEM)
    devices = groups * planes
    tile_shape = (spans * TOPK // LANES, 3 * LANES)
    results = pl.pallas_call(
        functools.partial(exchange_kernel, groups, planes),
        out_shape=[pltpu.VMEM(momentum.shape, jnp.bfloat16)] * 2,
        in_specs=[anywhere] * len(operands),
        out_specs=[vmem] * 2,
        scratch_shapes=[pltpu.SMEM(owner_span_order.shape, jnp.int32)]
        + [pltpu.VMEM(x.shape, x.dtype) for x in operands[1:]]
        + [
            pltpu.VMEM((devices, *tile_shape), jnp.bfloat16),
            pltpu.VMEM((LANES // TOPK, *tile_shape), jnp.bfloat16),
            pltpu.VMEM((spans, BLOCK, LANES), jnp.float32),
            pltpu.VMEM((chunks * spans, LANES), jnp.float32),
            pltpu.SemaphoreType.DMA((len(operands),)),
            pltpu.SemaphoreType.DMA,
            pltpu.SemaphoreType.DMA((planes,)),
        ],
        compiler_params=pltpu.CompilerParams(collective_id=0, has_side_effects=True),
    )(*operands)
    return pl.pallas_call(
        store_kernel,
        out_shape=[jax.ShapeDtypeStruct(momentum.shape, jnp.bfloat16)] * 2,
        in_specs=[vmem] * 2,
        out_specs=[anywhere] * 2,
        scratch_shapes=[pltpu.SemaphoreType.DMA((2,))],
    )(*[pltpu.with_memory_space_constraint(result, pltpu.VMEM) for result in results])


def local(groups, planes, momentum, picked, owner_span_order):
    entries = momentum.shape[0] * TOPK
    if entries % LANES == 0 and groups % (LANES // TOPK) == 0 and groups * planes * entries * 8 <= GATHER_BYTES:
        return local_small(groups, planes, momentum, picked, owner_span_order)
    return local_large(momentum, picked, owner_span_order)


def solution(mesh):
    return jax.shard_map(
        functools.partial(local, mesh.shape["grp"], mesh.shape["rep"]),
        mesh=mesh,
        in_specs=(P(("grp", "rep"), None), P(("grp", "rep"), None), P()),
        out_specs=(P(), P(("grp", "rep"), None)),
        check_vma=False,
    )
```

profile of v0, /device:TPU:0, one launch (start us, length us, event | category | flops | bytes accessed | tf_op | source)
XLA Modules:
  0.0 12.3 jit_solution(9132161292089090562)
XLA Ops:
  0.6 11.0 %shard_map.86 = (bf16[8,4096]{1,0:T(8,128)(2,1)S(1)}, bf16[8,4096]{1,0:T(8,128)(2,1)S(1)}) custom-call(s32[8]{0:T(128)} %order_hbm.1, bf16[8,4096]{1,0:T(8,128)(2,1)} %momentum_hbm.1, s32[8,32]{1,0:T(8,128)} %picked_hbm.1, bf16[512,64]{1,0:T(8,128)(2,1)} %constant.8.clone.rows_hbm, bf16[64,64]{1,0:T(8,128)(2,1)} %constant.9.clone.cols_hbm, ...), custom_call_target="tpu_custom_call" | custom-call | tf_op jit(solution)/shard_map/pallas_call | solution.py:337
  11.6 0.7 %shard_map.87 = (bf16[8,4096]{1,0:T(8,128)(2,1)}, bf16[8,4096]{1,0:T(8,128)(2,1)}) custom-call(bf16[8,4096]{1,0:T(8,128)(2,1)S(1)} %get-tuple-element.4.update_ref, bf16[8,4096]{1,0:T(8,128)(2,1)S(1)} %get-tuple-element.5.residual_ref), custom_call_target="tpu_custom_call" | custom-call | tf_op jit(solution)/shard_map/pallas_call | solution.py:355
where the time goes:
time: 12.4 us; the launch traced here: 12.3 us
  Pallas kernels  11.6 us (94%)
  between operations  0.64 us (5%)
    pallas_call x1, Pallas kernels, local_small(): pl.pallas_call(functools.partial(exchange_kernel, groups, planes), out_sh...  11 us
    pallas_call x1, Pallas kernels, local_small(): pl.pallas_call(store_kernel, out_shape=[jax.ShapeDtypeStruct(momentum.sha...  0.67 us

commit v1 on v0

v1 whole, which is shorter than its diff:
```python
import math

import functools

import jax
import jax.numpy as jnp
from jax import lax
from jax.experimental import pallas as pl
from jax.experimental.pallas import tpu as pltpu
from jax.sharding import PartitionSpec as P

BLOCK = 64
TOPK = 32
CH_OWN = 1


def dct_cosines(points):
    freq = jnp.arange(points, dtype=jnp.float32)[:, None]
    place = jnp.arange(points, dtype=jnp.float32)[None, :]
    values = jnp.cos(jnp.pi * (2.0 * place + 1.0) * freq / (2.0 * points)) * jnp.sqrt(2.0 / points)
    values = values.at[0].multiply(jnp.sqrt(0.5))
    rounded = lax.optimization_barrier(values.astype(jnp.bfloat16))
    return rounded.astype(jnp.float32)


def forward(square_low, cosines, cos_low):
    half = jnp.einsum("cab,jb->caj", square_low, cos_low, preferred_element_type=jnp.float32)
    return jnp.einsum("ia,caj->cij", cosines, half, precision=lax.Precision.HIGHEST)


def decode(dense_matrix, cosines):
    square = dense_matrix.reshape(dense_matrix.shape[0], BLOCK, BLOCK)
    half = jnp.einsum("cij,jb->cib", square, cosines, precision=lax.Precision.HIGHEST)
    full = jnp.einsum("ia,cib->cab", cosines, half, precision=lax.Precision.HIGHEST)
    return full.reshape(dense_matrix.shape[0], BLOCK * BLOCK)


def decode_sparse(dense_low, cosines, cos_low):
    square = dense_low.reshape(dense_low.shape[0], BLOCK, BLOCK)
    half = jnp.einsum("cij,jb->cib", square, cos_low, preferred_element_type=jnp.float32)
    full = jnp.einsum("ia,cib->cab", cosines, half, precision=lax.Precision.HIGHEST)
    return full.reshape(dense_low.shape[0], BLOCK * BLOCK)


def densify(values, spots):
    entries, columns = values.shape
    per_step = math.gcd(entries, max(1, 65536 // columns))
    positions = jnp.arange(BLOCK, dtype=jnp.int32)

    def one_block(pieces):
        block_values, block_spots = pieces
        zeros = jnp.zeros_like(block_values)
        row_onehot = jnp.where(
            (block_spots // BLOCK)[:, None, :] == positions[None, :, None],
            block_values[:, None, :],
            zeros[:, None, :],
        )
        column_onehot = ((block_spots % BLOCK)[:, None, :] == positions[None, :, None]).astype(
            jnp.bfloat16
        )
        dense_matrix = jnp.einsum(
            "bcy,bzy->bcz", row_onehot, column_onehot, preferred_element_type=jnp.float32
        )
        return dense_matrix.reshape(per_step, BLOCK * BLOCK)

    stacked = lax.map(
        one_block,
        (
            values.reshape(entries // per_step, per_step, columns),
            spots.reshape(entries // per_step, per_step, columns),
        ),
    )
    return stacked.reshape(entries, BLOCK * BLOCK)


def owner_sum(received):
    values, spots = received
    return densify(values[0], spots[0])


def local_large(momentum, picked, owner_span_order):
    cosines = dct_cosines(BLOCK)
    cos_low = cosines.astype(jnp.bfloat16)
    owners = lax.axis_size("grp")
    span_count = momentum.shape[0]
    square_low = momentum.reshape(span_count, BLOCK, BLOCK)
    transform_coefficients = forward(square_low, cosines, cos_low).reshape(
        span_count, BLOCK * BLOCK
    )
    chosen = jnp.take_along_axis(transform_coefficients, picked, axis=1).astype(jnp.bfloat16)
    own_dense = densify(chosen, picked).astype(jnp.bfloat16)
    residual_momentum = (
        momentum.astype(jnp.float32) - decode_sparse(own_dense, cosines, cos_low)
    ).astype(jnp.bfloat16)
    slot_values = jnp.take(chosen, owner_span_order, axis=0)
    slot_spots = jnp.take(picked, owner_span_order, axis=0)
    shaped = (slot_values.reshape(owners, CH_OWN, TOPK), slot_spots.reshape(owners, CH_OWN, TOPK))
    partial_sum = owner_sum(
        (
            lax.all_to_all(shaped[0], "grp", split_axis=0, concat_axis=2, tiled=True),
            lax.all_to_all(shaped[1], "grp", split_axis=0, concat_axis=2, tiled=True),
        )
    )
    partial_sum = lax.psum(partial_sum, "rep")
    my_share = decode(partial_sum, cosines).astype(jnp.bfloat16)
    update = lax.all_gather(my_share, "grp", axis=0, tiled=True)
    return (update, residual_momentum)


LANES = 128
LOADS = 4
GATHER_BYTES = 2**20


def cosines_at(freq, place):
    turn = (freq * (2 * place + 1)) & (4 * BLOCK - 1)
    turn = jnp.where(turn > 2 * BLOCK, 4 * BLOCK - turn, turn)
    past = turn > BLOCK
    turn = jnp.where(past, 2 * BLOCK - turn, turn)
    angle = turn.astype(jnp.float32) * (math.pi / (2 * BLOCK))
    square = angle * angle
    value = jnp.full(square.shape, 1 / math.factorial(12), jnp.float32)
    for power in (10, 8, 6, 4, 2, 0):
        value = (-1) ** (power // 2) / math.factorial(power) + square * value
    scale = jnp.where(freq == 0, math.sqrt(1 / BLOCK), math.sqrt(2 / BLOCK))
    return (jnp.where(past, -value, value) * scale).astype(jnp.bfloat16)


def contract_lanes(left, right):
    return lax.dot_general(
        left, right, (((1,), (1,)), ((), ())), preferred_element_type=jnp.float32
    )


def matmul(left, right):
    return jnp.dot(left, right, preferred_element_type=jnp.float32)


def split(value):
    high = value.astype(jnp.bfloat16)
    return high, (value - high.astype(jnp.float32)).astype(jnp.bfloat16)


def exchange_kernel(
    groups,
    planes,
    order_hbm,
    momentum_hbm,
    picked_hbm,
    update_ref,
    residual_ref,
    order_ref,
    momentum_ref,
    picked_ref,
    rows_ref,
    cols_ref,
    twice_ref,
    pairs_ref,
    message,
    box,
    decoded,
    load_sem,
    send_sem,
    recv_sem,
    all_here,
):
    pltpu.make_async_copy(picked_hbm, picked_ref, load_sem.at[0]).start()
    pltpu.make_async_copy(order_hbm, order_ref, load_sem.at[1]).start()
    width = momentum_ref.shape[1] // LOADS
    for n in range(LOADS):
        piece = pl.ds(n * width, width)
        pltpu.make_async_copy(momentum_hbm.at[:, piece], momentum_ref.at[:, piece], load_sem.at[2]).start()
    spans = momentum_ref.shape[0]
    entries = spans * TOPK
    chunks = BLOCK * BLOCK // LANES
    folds = chunks // 2
    in_tile = LANES // TOPK
    tiles = entries // LANES
    halves = groups // in_tile
    devices = groups * planes
    my_group, my_plane = lax.axis_index("grp"), lax.axis_index("rep")
    group_of = [lax.rem(my_group + step, groups) for step in range(groups)]
    plane_of = [lax.rem(my_plane + step, planes) for step in range(planes)]
    first = {"grp": jnp.int32(0), "rep": jnp.int32(0)}
    second = {"grp": jnp.int32(1), "rep": jnp.int32(0)}
    is_first = jnp.logical_and(my_plane == 0, my_group == 0)
    is_second = jnp.logical_and(my_plane == 0, my_group == 1)
    last = {"grp": jnp.int32(groups - 1), "rep": jnp.int32(planes - 1)}
    is_last = jnp.logical_and(my_plane == planes - 1, my_group == groups - 1)
    is_early = jnp.logical_or(is_first, is_second)
    peers = [{"grp": group_of[g], "rep": plane_of[z]} for z in range(planes) for g in range(groups) if z or g]
    peers = peers[groups - 1 :] + peers[: groups - 1]
    barrier = pltpu.get_barrier_semaphore()

    def signal(semaphore, peer):
        pl.semaphore_signal(semaphore, inc=1, device_id=peer, device_id_type=pl.DeviceIdType.MESH)

    @pl.when(is_early)
    def _():
        for peer in peers:
            signal(barrier, peer)

    @pl.when(jnp.logical_not(jnp.logical_or(is_early, is_last)))
    def _():
        signal(barrier, last)

    def iotas(shape):
        return [lax.broadcasted_iota(jnp.int32, shape, d) for d in range(2)]

    line, freq = iotas((2 * folds * spans, BLOCK))
    place = 2 * (line % (folds * spans) // spans) + line // (folds * spans)
    rows_ref[...] = cosines_at(freq, place)
    line, freq = iotas((BLOCK, BLOCK))
    cols_ref[...] = cosines_at(freq, line)
    pairs_ref[...] = cosines_at(freq, 2 * (line % chunks) + line // chunks)
    line, place = iotas((BLOCK, LANES))
    twice_ref[...] = cosines_at(line, place % BLOCK)

    span, lane = iotas((spans, entries))
    turn = lax.rem(my_group, in_tile)
    block = (lane % LANES) // TOPK + in_tile - turn
    slot = lane // LANES * in_tile + jnp.where(block >= in_tile, block - in_tile, block)
    pltpu.make_async_copy(picked_hbm, picked_ref, load_sem.at[0]).wait()
    pltpu.make_async_copy(order_hbm, order_ref, load_sem.at[1]).wait()
    sent = jnp.full(slot.shape, order_ref[0])
    for s in range(1, spans):
        sent = jnp.where(slot == s, order_ref[s], sent)
    mine = span == sent
    spread = jnp.concatenate([picked_ref[...]] * spans, axis=1)
    spots = jnp.sum(jnp.where(mine, spread, 0), axis=0, keepdims=True)
    freq = lax.broadcasted_iota(jnp.int32, (BLOCK, entries), 0)
    row_spot, col_spot = spots // BLOCK, spots % BLOCK
    one_row = jnp.where(freq == row_spot, 1.0, 0.0).astype(jnp.bfloat16)
    one_col = jnp.where(freq == col_spot, 1.0, 0.0).astype(jnp.bfloat16)
    odd = jnp.where(row_spot % 2 == 1, -1.0, 1.0)
    wave = matmul(cols_ref[...], one_col)
    mirror = (wave * odd).astype(jnp.bfloat16)
    wave = wave.astype(jnp.bfloat16)
    blank = jnp.zeros_like(wave)
    waves = [
        jnp.concatenate([wave, blank, blank, mirror], axis=0),
        jnp.concatenate([blank, wave, mirror, blank], axis=0),
    ]
    half_rows = folds * spans
    row_waves = [matmul(rows_ref[p * half_rows : (p + 1) * half_rows, :], one_row) for p in range(2)]

    def by_tile(row):
        return jnp.concatenate(
            [row[:, h * LANES : (h + 1) * LANES] for h in range(tiles)], axis=0
        ).astype(jnp.bfloat16)

    message[:, LANES : 2 * LANES] = by_tile(row_spot.astype(jnp.float32))
    message[:, 2 * LANES :] = by_tile(col_spot.astype(jnp.float32))

    @pl.when(is_last)
    def _():
        pl.semaphore_wait(barrier, devices - 1)
        for peer in peers:
            signal(all_here, peer)

    pltpu.make_async_copy(momentum_hbm, momentum_ref, load_sem.at[2]).wait()

    def chunk(k):
        return momentum_ref[:, k * LANES : (k + 1) * LANES].astype(jnp.float32)

    def folded():
        return jnp.concatenate(
            [
                jnp.concatenate([chunk(k) for k in range(folds)], axis=0),
                jnp.concatenate([chunk(chunks - 1 - k) for k in range(folds)], axis=0),
            ],
            axis=1,
        )

    momentum_low = folded().astype(jnp.bfloat16)
    total = jnp.zeros((spans, entries), jnp.float32)
    for p in range(2):
        product = row_waves[p] * matmul(momentum_low, waves[p])
        total += jnp.sum(product.reshape(folds, spans, entries), axis=0)
    chosen = jnp.sum(jnp.where(mine, total, 0.0), axis=0, keepdims=True)
    message[:, :LANES] = by_tile(chosen)
    me = my_plane * groups + my_group
    landing = recv_sem.at[my_plane * halves + my_group // in_tile]

    def send(peer):
        copy = pltpu.make_async_remote_copy(
            src_ref=message,
            dst_ref=box.at[me],
            send_sem=send_sem,
            recv_sem=landing,
            device_id=peer,
            device_id_type=pl.DeviceIdType.MESH,
        )
        return copy

    @pl.when(jnp.logical_not(is_last))
    def _():
        pl.semaphore_wait(barrier, jnp.where(is_early, 1, 2))

    pl.when(jnp.logical_not(is_first))(lambda: send(first).start())
    pl.when(jnp.logical_not(is_second))(lambda: send(second).start())
    pltpu.make_async_copy(message, box.at[me], landing).start()

    chosen = chosen.astype(jnp.bfloat16).astype(jnp.float32)
    scaled = jnp.where(mine, chosen, 0.0)
    residual = folded()
    for p in range(2):
        weight = row_waves[p].reshape(folds, spans, entries) * scaled[None]
        for part in split(weight.reshape(half_rows, entries)):
            residual -= contract_lanes(part, waves[p])
    for k in range(folds):
        for n, at in enumerate((k, chunks - 1 - k)):
            residual_ref[:, at * LANES : (at + 1) * LANES] = residual[
                k * spans : (k + 1) * spans, n * LANES : (n + 1) * LANES
            ].astype(jnp.bfloat16)

    @pl.when(jnp.logical_not(is_last))
    def _():
        pl.semaphore_wait(all_here, 1)

    for z in reversed(range(planes)):
        for g in range(groups):
            if z:
                peer = {"grp": group_of[g], "rep": jnp.int32(z)}
                if g:
                    send(peer).start()
                else:
                    pl.when(my_plane != z)(lambda peer=peer: send(peer).start())
            elif g > 1:
                peer = {"grp": jnp.int32(g), "rep": jnp.int32(0)}
                pl.when(jnp.logical_or(my_plane != 0, my_group != g))(lambda peer=peer: send(peer).start())

    block = lax.broadcasted_iota(jnp.int32, (tiles, LANES), 1) // TOPK
    taken = [block == turn for turn in range(in_tile)]
    one, zero = jnp.ones((), jnp.bfloat16), jnp.zeros((), jnp.bfloat16)

    def arrived(z, half):
        first = z * groups + half * in_tile
        landed = box.at[pl.ds(first, in_tile)]
        pltpu.make_async_copy(landed, landed, recv_sem.at[z * halves + half]).wait()
        slots = [box[first + n].astype(jnp.float32) for n in range(in_tile)]
        return [[slot[:, n * LANES : (n + 1) * LANES] for slot in slots] for n in range(3)]

    def span_rows(parts, c):
        row = parts[0]
        for turn in range(1, in_tile):
            row = jnp.where(taken[(c + turn) % in_tile], parts[turn], row)
        return row

    plane_at = [jnp.where(2 * my_plane < planes, z, planes - 1 - z) for z in range(planes)]
    grouped = [[(z, half) for half in range(halves)] for z in plane_at[:-1]]
    grouped += [[(plane_at[-1], half)] for half in range(halves)]
    sums = [None] * spans
    for group in grouped:
        pieces = [arrived(z, half) for z, half in group]
        freq = lax.broadcasted_iota(jnp.int32, (BLOCK, len(group) * LANES), 0)
        freq = freq.astype(jnp.float32).astype(jnp.bfloat16)
        for c in range(in_tile):
            value, row, column = (
                jnp.concatenate([span_rows(piece[n], c) for piece in pieces], axis=1).astype(jnp.bfloat16)
                for n in range(3)
            )
            for h in range(tiles):
                left = jnp.where(freq == row[h : h + 1], one, zero)
                right = jnp.where(freq == column[h : h + 1], value[h : h + 1], zero)
                part = contract_lanes(left, right)
                s = h * in_tile + c
                sums[s] = part if sums[s] is None else sums[s] + part
    lower = lax.broadcasted_iota(jnp.int32, (chunks, LANES), 1) < BLOCK
    dense = [matmul(part.astype(jnp.bfloat16), twice_ref[...]).astype(jnp.bfloat16) for part in sums]
    for s in range(spans):
        full = matmul(pairs_ref[...], dense[s])
        decoded[pl.ds(s, chunks, stride=spans), :] = jnp.where(lower, full[:chunks], full[chunks:])
    for k in range(chunks):
        update_ref[:, k * LANES : (k + 1) * LANES] = decoded[
            k * spans : (k + 1) * spans, :
        ].astype(jnp.bfloat16)
    for _ in range(devices - 1):
        send(first).wait_send()


def store_kernel(update_ref, residual_ref, update_hbm, residual_hbm, sem):
    stores = [
        pltpu.make_async_copy(residual_ref, residual_hbm, sem.at[0]),
        pltpu.make_async_copy(update_ref, update_hbm, sem.at[1]),
    ]
    for store in stores:
        store.start()
    for store in stores:
        store.wait()


def local_small(groups, planes, momentum, picked, owner_span_order):
    spans = momentum.shape[0]
    chunks = BLOCK * BLOCK // LANES
    operands = [owner_span_order, momentum, picked]
    anywhere = pl.BlockSpec(memory_space=pl.ANY)
    vmem = pl.BlockSpec(memory_space=pltpu.VMEM)
    devices = groups * planes
    tile_shape = (spans * TOPK // LANES, 3 * LANES)
    results = pl.pallas_call(
        functools.partial(exchange_kernel, groups, planes),
        out_shape=[pltpu.VMEM(momentum.shape, jnp.bfloat16)] * 2,
        in_specs=[anywhere] * len(operands),
        out_specs=[vmem] * 2,
        scratch_shapes=[
            pltpu.SMEM(owner_span_order.shape, jnp.int32),
            pltpu.VMEM(momentum.shape, momentum.dtype),
            pltpu.VMEM(picked.shape, picked.dtype),
            pltpu.VMEM((chunks * spans, BLOCK), jnp.bfloat16),
            pltpu.VMEM((BLOCK, BLOCK), jnp.bfloat16),
            pltpu.VMEM((BLOCK, LANES), jnp.bfloat16),
            pltpu.VMEM((BLOCK, BLOCK), jnp.bfloat16),
            pltpu.VMEM(tile_shape, jnp.bfloat16),
            pltpu.VMEM((devices, *tile_shape), jnp.bfloat16),
            pltpu.VMEM((chunks * spans, LANES), jnp.float32),
            pltpu.SemaphoreType.DMA((3,)),
            pltpu.SemaphoreType.DMA,
            pltpu.SemaphoreType.DMA((devices * TOPK // LANES,)),
            pltpu.SemaphoreType.REGULAR,
        ],
        compiler_params=pltpu.CompilerParams(collective_id=0, has_side_effects=True),
    )(*operands)
    return pl.pallas_call(
        store_kernel,
        out_shape=[jax.ShapeDtypeStruct(momentum.shape, jnp.bfloat16)] * 2,
        in_specs=[vmem] * 2,
        out_specs=[anywhere] * 2,
        scratch_shapes=[pltpu.SemaphoreType.DMA((2,))],
    )(*[pltpu.with_memory_space_constraint(result, pltpu.VMEM) for result in results])


def local(groups, planes, momentum, picked, owner_span_order):
    entries = momentum.shape[0] * TOPK
    if entries % LANES == 0 and groups % (LANES // TOPK) == 0 and groups * planes * entries * 8 <= GATHER_BYTES:
        return local_small(groups, planes, momentum, picked, owner_span_order)
    return local_large(momentum, picked, owner_span_order)


def solution(mesh):
    return jax.shard_map(
        functools.partial(local, mesh.shape["grp"], mesh.shape["rep"]),
        mesh=mesh,
        in_specs=(P(("grp", "rep"), None), P(("grp", "rep"), None), P()),
        out_specs=(P(), P(("grp", "rep"), None)),
        check_vma=False,
    )
```

time: 12.4 us -> 11.9 us (0.960)
  Pallas kernels: 11.6 us -> 11.1 us
    pallas_call x1, Pallas kernels: 11 us -> 10.4 us  [local_small(): pl.pallas_call(functools.partial(exchange_kernel, groups, planes), out_sh...]
where the time goes in v1:
time: 11.9 us; the launch traced here: 11.7 us
  Pallas kernels  11.1 us (93%)
  between operations  0.64 us (5%)
    pallas_call x1, Pallas kernels, local_small(): pl.pallas_call(functools.partial(exchange_kernel, groups, planes), out_sh...  10.4 us
    pallas_call x1, Pallas kernels, local_small(): pl.pallas_call(store_kernel, out_shape=[jax.ShapeDtypeStruct(momentum.sha...  0.67 us

profile of v1, /device:TPU:0, one launch (start us, length us, event | category | flops | bytes accessed | tf_op | source)
XLA Modules:
  0.0 11.7 jit_solution(10809370197784803701)
XLA Ops:
  0.6 10.4 %shard_map.50 = (bf16[8,4096]{1,0:T(8,128)(2,1)S(1)}, bf16[8,4096]{1,0:T(8,128)(2,1)S(1)}) custom-call(s32[8]{0:T(128)} %order_hbm.1, bf16[8,4096]{1,0:T(8,128)(2,1)} %momentum_hbm.1, s32[8,32]{1,0:T(8,128)} %picked_hbm.1), custom_call_target="tpu_custom_call" | custom-call | tf_op jit(solution)/shard_map/pallas_call | solution.py:401
  11.1 0.7 %shard_map.51 = (bf16[8,4096]{1,0:T(8,128)(2,1)}, bf16[8,4096]{1,0:T(8,128)(2,1)}) custom-call(bf16[8,4096]{1,0:T(8,128)(2,1)S(1)} %get-tuple-element.4.update_ref, bf16[8,4096]{1,0:T(8,128)(2,1)S(1)} %get-tuple-element.5.residual_ref), custom_call_target="tpu_custom_call" | custom-call | tf_op jit(solution)/shard_map/pallas_call | solution.py:424

commit v2 on v1

--- a/solution.py
+++ b/solution.py
@@ -109,6 +109,7 @@
 
 LANES = 128
 LOADS = 4
+EARLY = 2
 GATHER_BYTES = 2**20
 
 
@@ -153,11 +154,12 @@
     momentum_ref,
     picked_ref,
     rows_ref,
-    cols_ref,
+    wide_ref,
     twice_ref,
     pairs_ref,
     message,
     box,
+    dense,
     decoded,
     load_sem,
     send_sem,
@@ -180,16 +182,20 @@
     devices = groups * planes
     my_group, my_plane = lax.axis_index("grp"), lax.axis_index("rep")
     group_of = [lax.rem(my_group + step, groups) for step in range(groups)]
-    plane_of = [lax.rem(my_plane + step, planes) for step in range(planes)]
-    first = {"grp": jnp.int32(0), "rep": jnp.int32(0)}
-    second = {"grp": jnp.int32(1), "rep": jnp.int32(0)}
-    is_first = jnp.logical_and(my_plane == 0, my_group == 0)
-    is_second = jnp.logical_and(my_plane == 0, my_group == 1)
+    early = max(1, planes * EARLY // 4)
     last = {"grp": jnp.int32(groups - 1), "rep": jnp.int32(planes - 1)}
     is_last = jnp.logical_and(my_plane == planes - 1, my_group == groups - 1)
-    is_early = jnp.logical_or(is_first, is_second)
-    peers = [{"grp": group_of[g], "rep": plane_of[z]} for z in range(planes) for g in range(groups) if z or g]
-    peers = peers[groups - 1 :] + peers[: groups - 1]
+    is_early = my_plane < early
+
+    def each_peer(lowest, highest, action):
+        for z in range(lowest, highest):
+            for g in range(groups):
+                peer = {"grp": group_of[g], "rep": jnp.int32(z)}
+                if g:
+                    action(peer)
+                else:
+                    pl.when(my_plane != z)(functools.partial(action, peer))
+
     barrier = pltpu.get_barrier_semaphore()
 
     def signal(semaphore, peer):
@@ -197,8 +203,7 @@
 
     @pl.when(is_early)
     def _():
-        for peer in peers:
-            signal(barrier, peer)
+        each_peer(0, planes, functools.partial(signal, barrier))
 
     @pl.when(jnp.logical_not(jnp.logical_or(is_early, is_last)))
     def _():
@@ -207,33 +212,50 @@
     def iotas(shape):
         return [lax.broadcasted_iota(jnp.int32, shape, d) for d in range(2)]
 
-    line, freq = iotas((2 * folds * spans, BLOCK))
-    place = 2 * (line % (folds * spans) // spans) + line // (folds * spans)
-    rows_ref[...] = cosines_at(freq, place)
+    line, freq = iotas((2 * folds, LANES))
+    table = cosines_at(freq % BLOCK, 2 * (line % folds) + line // folds).astype(jnp.float32)
+    for k in range(2 * folds):
+        rows_ref[k * spans : (k + 1) * spans, :] = jnp.broadcast_to(table[k : k + 1], (spans, LANES))
     line, freq = iotas((BLOCK, BLOCK))
-    cols_ref[...] = cosines_at(freq, line)
     pairs_ref[...] = cosines_at(freq, 2 * (line % chunks) + line // chunks)
     line, place = iotas((BLOCK, LANES))
     twice_ref[...] = cosines_at(line, place % BLOCK)
+    wide_ref[...] = cosines_at(place % BLOCK, line).astype(jnp.float32)
 
     span, lane = iotas((spans, entries))
     turn = lax.rem(my_group, in_tile)
     block = (lane % LANES) // TOPK + in_tile - turn
     slot = lane // LANES * in_tile + jnp.where(block >= in_tile, block - in_tile, block)
+    mine = span == slot
+
+    @pl.when(is_last)
+    def _():
+        pl.semaphore_wait(barrier, devices - 1)
+        each_peer(0, planes, functools.partial(signal, all_here))
+
     pltpu.make_async_copy(picked_hbm, picked_ref, load_sem.at[0]).wait()
-    pltpu.make_async_copy(order_hbm, order_ref, load_sem.at[1]).wait()
-    sent = jnp.full(slot.shape, order_ref[0])
-    for s in range(1, spans):
-        sent = jnp.where(slot == s, order_ref[s], sent)
-    mine = span == sent
     spread = jnp.concatenate([picked_ref[...]] * spans, axis=1)
+    pltpu.make_async_copy(momentum_hbm, momentum_ref, load_sem.at[2]).wait()
     spots = jnp.sum(jnp.where(mine, spread, 0), axis=0, keepdims=True)
-    freq = lax.broadcasted_iota(jnp.int32, (BLOCK, entries), 0)
     row_spot, col_spot = spots // BLOCK, spots % BLOCK
-    one_row = jnp.where(freq == row_spot, 1.0, 0.0).astype(jnp.bfloat16)
-    one_col = jnp.where(freq == col_spot, 1.0, 0.0).astype(jnp.bfloat16)
+
+    def looked_up(table, spot):
+        height = table.shape[0]
+        return jnp.concatenate(
+            [
+                jnp.take_along_axis(
+                    table,
+                    jnp.broadcast_to(spot[:, h * LANES : (h + 1) * LANES], (height, LANES)),
+                    axis=1,
+                    mode="promise_in_bounds",
+                )
+                for h in range(tiles)
+            ],
+            axis=1,
+        )
+
     odd = jnp.where(row_spot % 2 == 1, -1.0, 1.0)
-    wave = matmul(cols_ref[...], one_col)
+    wave = looked_up(wide_ref[...], col_spot)
     mirror = (wave * odd).astype(jnp.bfloat16)
     wave = wave.astype(jnp.bfloat16)
     blank = jnp.zeros_like(wave)
@@ -242,7 +264,7 @@
         jnp.concatenate([blank, wave, mirror, blank], axis=0),
     ]
     half_rows = folds * spans
-    row_waves = [matmul(rows_ref[p * half_rows : (p + 1) * half_rows, :], one_row) for p in range(2)]
+    row_waves = [looked_up(rows_ref[p * half_rows : (p + 1) * half_rows, :], row_spot) for p in range(2)]
 
     def by_tile(row):
         return jnp.concatenate(
@@ -251,14 +273,6 @@
 
     message[:, LANES : 2 * LANES] = by_tile(row_spot.astype(jnp.float32))
     message[:, 2 * LANES :] = by_tile(col_spot.astype(jnp.float32))
-
-    @pl.when(is_last)
-    def _():
-        pl.semaphore_wait(barrier, devices - 1)
-        for peer in peers:
-            signal(all_here, peer)
-
-    pltpu.make_async_copy(momentum_hbm, momentum_ref, load_sem.at[2]).wait()
 
     def chunk(k):
         return momentum_ref[:, k * LANES : (k + 1) * LANES].astype(jnp.float32)
@@ -282,8 +296,8 @@
     me = my_plane * groups + my_group
     landing = recv_sem.at[my_plane * halves + my_group // in_tile]
 
-    def send(peer):
-        copy = pltpu.make_async_remote_copy(
+    def copy_to(peer):
+        return pltpu.make_async_remote_copy(
             src_ref=message,
             dst_ref=box.at[me],
             send_sem=send_sem,
@@ -291,16 +305,18 @@
             device_id=peer,
             device_id_type=pl.DeviceIdType.MESH,
         )
-        return copy
+
+    def send(peer):
+        copy_to(peer).start()
 
     @pl.when(jnp.logical_not(is_last))
     def _():
-        pl.semaphore_wait(barrier, jnp.where(is_early, 1, 2))
-
-    pl.when(jnp.logical_not(is_first))(lambda: send(first).start())
-    pl.when(jnp.logical_not(is_second))(lambda: send(second).start())
+        pl.semaphore_wait(barrier, jnp.where(is_early, early * groups - 1, early * groups))
+
+    each_peer(0, early, send)
     pltpu.make_async_copy(message, box.at[me], landing).start()
 
+    pltpu.make_async_copy(order_hbm, order_ref, load_sem.at[1]).wait()
     chosen = chosen.astype(jnp.bfloat16).astype(jnp.float32)
     scaled = jnp.where(mine, chosen, 0.0)
     residual = folded()
@@ -318,17 +334,7 @@
     def _():
         pl.semaphore_wait(all_here, 1)
 
-    for z in reversed(range(planes)):
-        for g in range(groups):
-            if z:
-                peer = {"grp": group_of[g], "rep": jnp.int32(z)}
-                if g:
-                    send(peer).start()
-                else:
-                    pl.when(my_plane != z)(lambda peer=peer: send(peer).start())
-            elif g > 1:
-                peer = {"grp": jnp.int32(g), "rep": jnp.int32(0)}
-                pl.when(jnp.logical_or(my_plane != 0, my_group != g))(lambda peer=peer: send(peer).start())
+    each_peer(early, planes, send)
 
     block = lax.broadcasted_iota(jnp.int32, (tiles, LANES), 1) // TOPK
     taken = [block == turn for turn in range(in_tile)]
@@ -367,16 +373,17 @@
                 s = h * in_tile + c
                 sums[s] = part if sums[s] is None else sums[s] + part
     lower = lax.broadcasted_iota(jnp.int32, (chunks, LANES), 1) < BLOCK
-    dense = [matmul(part.astype(jnp.bfloat16), twice_ref[...]).astype(jnp.bfloat16) for part in sums]
     for s in range(spans):
-        full = matmul(pairs_ref[...], dense[s])
+        dense[s] = matmul(sums[s].astype(jnp.bfloat16), twice_ref[...]).astype(jnp.bfloat16)
+    for s in range(spans):
+        full = matmul(pairs_ref[...], dense[order_ref[s]])
         decoded[pl.ds(s, chunks, stride=spans), :] = jnp.where(lower, full[:chunks], full[chunks:])
     for k in range(chunks):
         update_ref[:, k * LANES : (k + 1) * LANES] = decoded[
             k * spans : (k + 1) * spans, :
         ].astype(jnp.bfloat16)
     for _ in range(devices - 1):
-        send(first).wait_send()
+        copy_to(last).wait_send()
 
 
 def store_kernel(update_ref, residual_ref, update_hbm, residual_hbm, sem):
@@ -407,12 +414,13 @@
             pltpu.SMEM(owner_span_order.shape, jnp.int32),
             pltpu.VMEM(momentum.shape, momentum.dtype),
             pltpu.VMEM(picked.shape, picked.dtype),
-            pltpu.VMEM((chunks * spans, BLOCK), jnp.bfloat16),
-            pltpu.VMEM((BLOCK, BLOCK), jnp.bfloat16),
+            pltpu.VMEM((chunks * spans, LANES), jnp.float32),
+            pltpu.VMEM((BLOCK, LANES), jnp.float32),
             pltpu.VMEM((BLOCK, LANES), jnp.bfloat16),
             pltpu.VMEM((BLOCK, BLOCK), jnp.bfloat16),
             pltpu.VMEM(tile_shape, jnp.bfloat16),
             pltpu.VMEM((devices, *tile_shape), jnp.bfloat16),
+            pltpu.VMEM((spans, BLOCK, LANES), jnp.bfloat16),
             pltpu.VMEM((chunks * spans, LANES), jnp.float32),
             pltpu.SemaphoreType.DMA((3,)),
             pltpu.SemaphoreType.DMA,

time: 11.9 us -> 11.8 us (level)
  no operation moved by 1% of the time
where the time goes in v2:
time: 11.8 us; the launch traced here: 11.6 us
  Pallas kernels  11 us (93%)
  between operations  0.64 us (5%)
    pallas_call x1, Pallas kernels, local_small(): pl.pallas_call(functools.partial(exchange_kernel, groups, planes), out_sh...  10.3 us
    pallas_call x1, Pallas kernels, local_small(): pl.pallas_call(store_kernel, out_shape=[jax.ShapeDtypeStruct(momentum.sha...  0.67 us

profile of v2, /device:TPU:0, one launch (start us, length us, event | category | flops | bytes accessed | tf_op | source)
XLA Modules:
  0.0 11.6 jit_solution(654965583557616658)
XLA Ops:
  0.6 10.3 %shard_map.50 = (bf16[8,4096]{1,0:T(8,128)(2,1)S(1)}, bf16[8,4096]{1,0:T(8,128)(2,1)S(1)}) custom-call(s32[8]{0:T(128)} %order_hbm.1, bf16[8,4096]{1,0:T(8,128)(2,1)} %momentum_hbm.1, s32[8,32]{1,0:T(8,128)} %picked_hbm.1), custom_call_target="tpu_custom_call" | custom-call | tf_op jit(solution)/shard_map/pallas_call | solution.py:408
  11.0 0.7 %shard_map.51 = (bf16[8,4096]{1,0:T(8,128)(2,1)}, bf16[8,4096]{1,0:T(8,128)(2,1)}) custom-call(bf16[8,4096]{1,0:T(8,128)(2,1)S(1)} %get-tuple-element.4.update_ref, bf16[8,4096]{1,0:T(8,128)(2,1)S(1)} %get-tuple-element.5.residual_ref), custom_call_target="tpu_custom_call" | custom-call | tf_op jit(solution)/shard_map/pallas_call | solution.py:432

commit v3 on v2

--- a/solution.py
+++ b/solution.py
@@ -109,7 +109,6 @@
 
 LANES = 128
 LOADS = 4
-EARLY = 2
 GATHER_BYTES = 2**20
 
 
@@ -160,10 +159,16 @@
     message,
     box,
     dense,
+    summed,
+    partial,
+    row_side,
+    column_side,
+    weights,
     decoded,
     load_sem,
     send_sem,
     recv_sem,
+    spot_sem,
     all_here,
 ):
     pltpu.make_async_copy(picked_hbm, picked_ref, load_sem.at[0]).start()
@@ -182,19 +187,42 @@
     devices = groups * planes
     my_group, my_plane = lax.axis_index("grp"), lax.axis_index("rep")
     group_of = [lax.rem(my_group + step, groups) for step in range(groups)]
-    early = max(1, planes * EARLY // 4)
+    early_planes, early_groups = max(1, planes // 2), max(1, groups // 2)
+    early = early_planes * early_groups
     last = {"grp": jnp.int32(groups - 1), "rep": jnp.int32(planes - 1)}
+    hubs = 2
+    is_hub = jnp.logical_and(my_plane == 0, my_group < hubs)
+    is_final = jnp.logical_and(my_plane == planes - 1, my_group >= groups - in_tile)
     is_last = jnp.logical_and(my_plane == planes - 1, my_group == groups - 1)
-    is_early = my_plane < early
-
-    def each_peer(lowest, highest, action):
-        for z in range(lowest, highest):
+    is_early = jnp.logical_and(my_plane < early_planes, my_group < early_groups)
+
+    def to_all(planes_of, groups_of, action):
+        for z in planes_of:
+            for g in groups_of:
+                peer = {"grp": jnp.int32(g), "rep": jnp.int32(z)}
+                is_me = jnp.logical_and(my_plane == z, my_group == g)
+                pl.when(jnp.logical_not(is_me))(functools.partial(action, peer))
+
+    def to_hubs(action):
+        to_all(range(1), range(hubs), action)
+
+    def to_others(action):
+        to_all(range(1), range(hubs, early_groups), action)
+        to_all(range(1, early_planes), range(early_groups), action)
+
+    def to_early(action):
+        to_hubs(action)
+        to_others(action)
+
+    def to_late(action):
+        for z in range(early_planes, planes):
             for g in range(groups):
                 peer = {"grp": group_of[g], "rep": jnp.int32(z)}
                 if g:
                     action(peer)
                 else:
                     pl.when(my_plane != z)(functools.partial(action, peer))
+        to_all(range(early_planes), range(early_groups, groups), action)
 
     barrier = pltpu.get_barrier_semaphore()
 
@@ -203,7 +231,8 @@
 
     @pl.when(is_early)
     def _():
-        each_peer(0, planes, functools.partial(signal, barrier))
+        to_late(functools.partial(signal, barrier))
+        to_early(functools.partial(signal, barrier))
 
     @pl.when(jnp.logical_not(jnp.logical_or(is_early, is_last)))
     def _():
@@ -213,9 +242,7 @@
         return [lax.broadcasted_iota(jnp.int32, shape, d) for d in range(2)]
 
     line, freq = iotas((2 * folds, LANES))
-    table = cosines_at(freq % BLOCK, 2 * (line % folds) + line // folds).astype(jnp.float32)
-    for k in range(2 * folds):
-        rows_ref[k * spans : (k + 1) * spans, :] = jnp.broadcast_to(table[k : k + 1], (spans, LANES))
+    rows_ref[...] = cosines_at(freq % BLOCK, 2 * (line % folds) + line // folds).astype(jnp.float32)
     line, freq = iotas((BLOCK, BLOCK))
     pairs_ref[...] = cosines_at(freq, 2 * (line % chunks) + line // chunks)
     line, place = iotas((BLOCK, LANES))
@@ -231,7 +258,8 @@
     @pl.when(is_last)
     def _():
         pl.semaphore_wait(barrier, devices - 1)
-        each_peer(0, planes, functools.partial(signal, all_here))
+        to_late(functools.partial(signal, all_here))
+        to_early(functools.partial(signal, all_here))
 
     pltpu.make_async_copy(picked_hbm, picked_ref, load_sem.at[0]).wait()
     spread = jnp.concatenate([picked_ref[...]] * spans, axis=1)
@@ -258,94 +286,112 @@
     wave = looked_up(wide_ref[...], col_spot)
     mirror = (wave * odd).astype(jnp.bfloat16)
     wave = wave.astype(jnp.bfloat16)
-    blank = jnp.zeros_like(wave)
-    waves = [
-        jnp.concatenate([wave, blank, blank, mirror], axis=0),
-        jnp.concatenate([blank, wave, mirror, blank], axis=0),
-    ]
+    waves = [jnp.concatenate([wave, mirror], axis=0), jnp.concatenate([mirror, wave], axis=0)]
     half_rows = folds * spans
-    row_waves = [looked_up(rows_ref[p * half_rows : (p + 1) * half_rows, :], row_spot) for p in range(2)]
+    row_wave = looked_up(rows_ref[...], row_spot)
+    row_waves = [row_wave[p * folds : (p + 1) * folds][:, None, :] for p in range(2)]
 
     def by_tile(row):
         return jnp.concatenate(
             [row[:, h * LANES : (h + 1) * LANES] for h in range(tiles)], axis=0
         ).astype(jnp.bfloat16)
 
-    message[:, LANES : 2 * LANES] = by_tile(row_spot.astype(jnp.float32))
-    message[:, 2 * LANES :] = by_tile(col_spot.astype(jnp.float32))
-
-    def chunk(k):
-        return momentum_ref[:, k * LANES : (k + 1) * LANES].astype(jnp.float32)
-
-    def folded():
-        return jnp.concatenate(
-            [
-                jnp.concatenate([chunk(k) for k in range(folds)], axis=0),
-                jnp.concatenate([chunk(chunks - 1 - k) for k in range(folds)], axis=0),
-            ],
-            axis=1,
-        )
-
-    momentum_low = folded().astype(jnp.bfloat16)
-    total = jnp.zeros((spans, entries), jnp.float32)
-    for p in range(2):
-        product = row_waves[p] * matmul(momentum_low, waves[p])
-        total += jnp.sum(product.reshape(folds, spans, entries), axis=0)
-    chosen = jnp.sum(jnp.where(mine, total, 0.0), axis=0, keepdims=True)
-    message[:, :LANES] = by_tile(chosen)
     me = my_plane * groups + my_group
-    landing = recv_sem.at[my_plane * halves + my_group // in_tile]
-
-    def copy_to(peer):
+    landing = my_plane * halves + my_group // in_tile
+    value_part, spot_part = pl.ds(0, LANES), pl.ds(LANES, 2 * LANES)
+
+    def copy_to(peer, lanes, semaphore):
         return pltpu.make_async_remote_copy(
-            src_ref=message,
-            dst_ref=box.at[me],
+            src_ref=message.at[:, lanes],
+            dst_ref=box.at[me, :, lanes],
             send_sem=send_sem,
-            recv_sem=landing,
+            recv_sem=semaphore,
             device_id=peer,
             device_id_type=pl.DeviceIdType.MESH,
         )
 
     def send(peer):
-        copy_to(peer).start()
-
-    @pl.when(jnp.logical_not(is_last))
-    def _():
-        pl.semaphore_wait(barrier, jnp.where(is_early, early * groups - 1, early * groups))
-
-    each_peer(0, early, send)
-    pltpu.make_async_copy(message, box.at[me], landing).start()
+        copy_to(peer, pl.ds(0, 3 * LANES), recv_sem.at[landing]).start()
+
+    def send_spots(peer):
+        copy_to(peer, spot_part, spot_sem).start()
+
+    def send_values(peer):
+        copy_to(peer, value_part, recv_sem.at[landing]).start()
+
+    message[:, LANES : 2 * LANES] = by_tile(row_spot.astype(jnp.float32))
+    message[:, 2 * LANES :] = by_tile(col_spot.astype(jnp.float32))
+    @pl.when(jnp.logical_and(is_final, jnp.logical_not(is_last)))
+    def _():
+        pl.semaphore_wait(barrier, early)
+
+    pl.when(is_final)(lambda: to_hubs(send_spots))
+
+    def chunk(k):
+        return momentum_ref[:, k * LANES : (k + 1) * LANES].astype(jnp.float32)
+
+    left_lanes = lax.broadcasted_iota(jnp.int32, (spans, LANES), 1) < BLOCK
+
+    def folded(p):
+        pairs = [(chunk(k), chunk(chunks - 1 - k)) for k in range(folds)]
+        return jnp.concatenate([jnp.where(left_lanes, pair[p], pair[1 - p]) for pair in pairs], axis=0)
+
+    total = jnp.zeros((spans, entries), jnp.float32)
+    for p in range(2):
+        product = matmul(folded(p).astype(jnp.bfloat16), waves[p]).reshape(folds, spans, entries)
+        total += jnp.sum(row_waves[p] * product, axis=0)
+    chosen = jnp.sum(jnp.where(mine, total, 0.0), axis=0, keepdims=True)
+    message[:, :LANES] = by_tile(chosen)
+
+    @pl.when(jnp.logical_not(is_final))
+    def _():
+        pl.semaphore_wait(barrier, jnp.where(is_early, early - 1, early))
+        to_hubs(send)
+
+    pl.when(is_final)(lambda: to_hubs(send_values))
+    to_others(send)
+
+    pltpu.make_async_copy(message, box.at[me], recv_sem.at[landing]).start()
 
     pltpu.make_async_copy(order_hbm, order_ref, load_sem.at[1]).wait()
     chosen = chosen.astype(jnp.bfloat16).astype(jnp.float32)
     scaled = jnp.where(mine, chosen, 0.0)
-    residual = folded()
+    residuals = []
     for p in range(2):
-        weight = row_waves[p].reshape(folds, spans, entries) * scaled[None]
+        weight = row_waves[p] * scaled[None]
+        residual = folded(p)
         for part in split(weight.reshape(half_rows, entries)):
             residual -= contract_lanes(part, waves[p])
+        residuals.append(residual)
     for k in range(folds):
+        pair = [residual[k * spans : (k + 1) * spans] for residual in residuals]
         for n, at in enumerate((k, chunks - 1 - k)):
-            residual_ref[:, at * LANES : (at + 1) * LANES] = residual[
-                k * spans : (k + 1) * spans, n * LANES : (n + 1) * LANES
-            ].astype(jnp.bfloat16)
+            residual_ref[:, at * LANES : (at + 1) * LANES] = jnp.where(
+                left_lanes, pair[n], pair[1 - n]
+            ).astype(jnp.bfloat16)
 
     @pl.when(jnp.logical_not(is_last))
     def _():
         pl.semaphore_wait(all_here, 1)
 
-    each_peer(early, planes, send)
+    to_late(send)
 
     block = lax.broadcasted_iota(jnp.int32, (tiles, LANES), 1) // TOPK
     taken = [block == turn for turn in range(in_tile)]
     one, zero = jnp.ones((), jnp.bfloat16), jnp.zeros((), jnp.bfloat16)
 
+    def await_part(z, half, lanes, semaphore):
+        landed = box.at[pl.ds(z * groups + half * in_tile, in_tile), :, lanes]
+        pltpu.make_async_copy(landed, landed, semaphore).wait()
+
+    def parts_of(z, half, part):
+        first = z * groups + half * in_tile
+        lanes = slice(part * LANES, (part + 1) * LANES)
+        return [box[first + n, :, lanes].astype(jnp.float32) for n in range(in_tile)]
+
     def arrived(z, half):
-        first = z * groups + half * in_tile
-        landed = box.at[pl.ds(first, in_tile)]
-        pltpu.make_async_copy(landed, landed, recv_sem.at[z * halves + half]).wait()
-        slots = [box[first + n].astype(jnp.float32) for n in range(in_tile)]
-        return [[slot[:, n * LANES : (n + 1) * LANES] for slot in slots] for n in range(3)]
+        await_part(z, half, pl.ds(0, 3 * LANES), recv_sem.at[z * halves + half])
+        return [parts_of(z, half, part) for part in range(3)]
 
     def span_rows(parts, c):
         row = parts[0]
@@ -354,36 +400,88 @@
         return row
 
     plane_at = [jnp.where(2 * my_plane < planes, z, planes - 1 - z) for z in range(planes)]
-    grouped = [[(z, half) for half in range(halves)] for z in plane_at[:-1]]
-    grouped += [[(plane_at[-1], half)] for half in range(halves)]
-    sums = [None] * spans
-    for group in grouped:
-        pieces = [arrived(z, half) for z, half in group]
-        freq = lax.broadcasted_iota(jnp.int32, (BLOCK, len(group) * LANES), 0)
+    grouped = [[(z, half) for half in range(halves)] for z in plane_at]
+    last_group = grouped.pop() if halves == 1 else [grouped[-1].pop()]
+
+    def spread_out(row, freq, fill):
+        return jnp.where(freq == row, fill, zero)
+
+    def add_up(groups_of, start):
+        sums = start
+        for group in groups_of:
+            if not group:
+                continue
+            pieces = [arrived(z, half) for z, half in group]
+            freq = lax.broadcasted_iota(jnp.int32, (BLOCK, len(group) * LANES), 0)
+            freq = freq.astype(jnp.float32).astype(jnp.bfloat16)
+            for c in range(in_tile):
+                value, row, column = (
+                    jnp.concatenate([span_rows(piece[n], c) for piece in pieces], axis=1).astype(jnp.bfloat16)
+                    for n in range(3)
+                )
+                for h in range(tiles):
+                    left = spread_out(row[h : h + 1], freq, one)
+                    right = spread_out(column[h : h + 1], freq, value[h : h + 1])
+                    part = contract_lanes(left, right)
+                    s = h * in_tile + c
+                    sums[s] = part if sums[s] is None else sums[s] + part
+        return sums
+
+    lower = lax.broadcasted_iota(jnp.int32, (chunks, LANES), 1) < BLOCK
+
+    def slot_matrices(sums):
+        for s in range(spans):
+            dense[s] = matmul(sums[s].astype(jnp.bfloat16), twice_ref[...]).astype(jnp.bfloat16)
+        for s in range(spans):
+            full = matmul(pairs_ref[...], dense[order_ref[s]])
+            yield s, jnp.where(lower, full[:chunks], full[chunks:])
+
+    for s, total in enumerate(add_up(grouped, [None] * spans)):
+        summed[s] = total
+
+    @pl.when(jnp.logical_not(is_hub))
+    def _():
+        for s, matrix in slot_matrices(add_up([last_group], [summed[s] for s in range(spans)])):
+            decoded[pl.ds(s, chunks, stride=spans), :] = matrix
+
+    @pl.when(is_hub)
+    def _():
+        for s, matrix in slot_matrices([summed[s] for s in range(spans)]):
+            partial[s] = matrix
+        final = (planes - 1, halves - 1)
+        await_part(*final, spot_part, spot_sem)
+        freq = lax.broadcasted_iota(jnp.int32, (BLOCK, entries), 0)
         freq = freq.astype(jnp.float32).astype(jnp.bfloat16)
+        rows, columns = (parts_of(*final, part) for part in (1, 2))
         for c in range(in_tile):
-            value, row, column = (
-                jnp.concatenate([span_rows(piece[n], c) for piece in pieces], axis=1).astype(jnp.bfloat16)
-                for n in range(3)
+            row, column = (
+                jnp.concatenate([span_rows(parts, c)[h : h + 1] for h in range(tiles)], axis=1).astype(jnp.bfloat16)
+                for parts in (rows, columns)
             )
+            left = matmul(pairs_ref[...], spread_out(row, freq, one)).astype(jnp.bfloat16)
+            right = matmul(wide_ref[:, :BLOCK].astype(jnp.bfloat16), spread_out(column, freq, one)).astype(jnp.bfloat16)
             for h in range(tiles):
-                left = jnp.where(freq == row[h : h + 1], one, zero)
-                right = jnp.where(freq == column[h : h + 1], value[h : h + 1], zero)
-                part = contract_lanes(left, right)
-                s = h * in_tile + c
-                sums[s] = part if sums[s] is None else sums[s] + part
-    lower = lax.broadcasted_iota(jnp.int32, (chunks, LANES), 1) < BLOCK
-    for s in range(spans):
-        dense[s] = matmul(sums[s].astype(jnp.bfloat16), twice_ref[...]).astype(jnp.bfloat16)
-    for s in range(spans):
-        full = matmul(pairs_ref[...], dense[order_ref[s]])
-        decoded[pl.ds(s, chunks, stride=spans), :] = jnp.where(lower, full[:chunks], full[chunks:])
+                row_side[h * in_tile + c] = left[:, h * LANES : (h + 1) * LANES]
+                column_side[h * in_tile + c] = right[:, h * LANES : (h + 1) * LANES]
+        await_part(*final, value_part, recv_sem.at[planes * halves - 1])
+        values = parts_of(*final, 0)
+        for c in range(in_tile):
+            value = span_rows(values, c)
+            for h in range(tiles):
+                weights[h * in_tile + c] = value[h : h + 1]
+        for s in range(spans):
+            span = order_ref[s]
+            left = row_side[span] * weights[span].astype(jnp.bfloat16)
+            right = column_side[span]
+            full = contract_lanes(left, jnp.concatenate([right, right], axis=0))
+            decoded[pl.ds(s, chunks, stride=spans), :] = partial[s] + jnp.where(lower, full[:chunks], full[chunks:])
+
     for k in range(chunks):
         update_ref[:, k * LANES : (k + 1) * LANES] = decoded[
             k * spans : (k + 1) * spans, :
         ].astype(jnp.bfloat16)
     for _ in range(devices - 1):
-        copy_to(last).wait_send()
+        copy_to(last, pl.ds(0, 3 * LANES), recv_sem.at[landing]).wait_send()
 
 
 def store_kernel(update_ref, residual_ref, update_hbm, residual_hbm, sem):
@@ -414,17 +512,23 @@
             pltpu.SMEM(owner_span_order.shape, jnp.int32),
             pltpu.VMEM(momentum.shape, momentum.dtype),
             pltpu.VMEM(picked.shape, picked.dtype),
-            pltpu.VMEM((chunks * spans, LANES), jnp.float32),
+            pltpu.VMEM((chunks, LANES), jnp.float32),
             pltpu.VMEM((BLOCK, LANES), jnp.float32),
             pltpu.VMEM((BLOCK, LANES), jnp.bfloat16),
             pltpu.VMEM((BLOCK, BLOCK), jnp.bfloat16),
             pltpu.VMEM(tile_shape, jnp.bfloat16),
             pltpu.VMEM((devices, *tile_shape), jnp.bfloat16),
             pltpu.VMEM((spans, BLOCK, LANES), jnp.bfloat16),
+            pltpu.VMEM((spans, BLOCK, BLOCK), jnp.float32),
+            pltpu.VMEM((spans, chunks, LANES), jnp.float32),
+            pltpu.VMEM((spans, BLOCK, LANES), jnp.bfloat16),
+            pltpu.VMEM((spans, BLOCK, LANES), jnp.bfloat16),
+            pltpu.VMEM((spans, 1, LANES), jnp.float32),
             pltpu.VMEM((chunks * spans, LANES), jnp.float32),
             pltpu.SemaphoreType.DMA((3,)),
             pltpu.SemaphoreType.DMA,
             pltpu.SemaphoreType.DMA((devices * TOPK // LANES,)),
+            pltpu.SemaphoreType.DMA,
             pltpu.SemaphoreType.REGULAR,
         ],
         compiler_params=pltpu.CompilerParams(collective_id=0, has_side_effects=True),
@@ -440,7 +544,7 @@
 
 def local(groups, planes, momentum, picked, owner_span_order):
     entries = momentum.shape[0] * TOPK
-    if entries % LANES == 0 and groups % (LANES // TOPK) == 0 and groups * planes * entries * 8 <= GATHER_BYTES:
+    if entries % LANES == 0 and planes > 1 and groups % (LANES // TOPK) == 0 and groups * planes * entries * 8 <= GATHER_BYTES:
         return local_small(groups, planes, momentum, picked, owner_span_order)
     return local_large(momentum, picked, owner_span_order)
 

time: 11.8 us -> 11.6 us (0.983)
  Pallas kernels: 11 us -> 10.8 us
    pallas_call x1, Pallas kernels: 10.3 us -> 10.1 us  [local_small(): pl.pallas_call(functools.partial(exchange_kernel, groups, planes), out_sh...]
where the time goes in v3:
time: 11.6 us; the launch traced here: 11.4 us
  Pallas kernels  10.8 us (93%)
  between operations  0.64 us (6%)
    pallas_call x1, Pallas kernels, local_small(): pl.pallas_call(functools.partial(exchange_kernel, groups, planes), out_sh...  10.1 us
    pallas_call x1, Pallas kernels, local_small(): pl.pallas_call(store_kernel, out_shape=[jax.ShapeDtypeStruct(momentum.sha...  0.67 us

profile of v3, /device:TPU:0, one launch (start us, length us, event | category | flops | bytes accessed | tf_op | source)
XLA Modules:
  0.0 11.4 jit_solution(4117583757339824798)
XLA Ops:
  0.6 10.1 %shard_map.50 = (bf16[8,4096]{1,0:T(8,128)(2,1)S(1)}, bf16[8,4096]{1,0:T(8,128)(2,1)S(1)}) custom-call(s32[8]{0:T(128)} %order_hbm.1, bf16[8,4096]{1,0:T(8,128)(2,1)} %momentum_hbm.1, s32[8,32]{1,0:T(8,128)} %picked_hbm.1), custom_call_target="tpu_custom_call" | custom-call | tf_op jit(solution)/shard_map/pallas_call | solution.py:506
  10.7 0.7 %shard_map.51 = (bf16[8,4096]{1,0:T(8,128)(2,1)}, bf16[8,4096]{1,0:T(8,128)(2,1)}) custom-call(bf16[8,4096]{1,0:T(8,128)(2,1)S(1)} %get-tuple-element.4.update_ref, bf16[8,4096]{1,0:T(8,128)(2,1)S(1)} %get-tuple-element.5.residual_ref), custom_call_target="tpu_custom_call" | custom-call | tf_op jit(solution)/shard_map/pallas_call | solution.py:536
